TPU v7x, 32 devices: a whole 2x2x4 slice. The times are simulated.
32 devices in a mesh: groups: 2 (over y), fsdp: 4 (over z), mp: 2 (over x), sub: 2 (over core).
Axes of the slice: x: 2, y: 2, z: 4, core: 2. Of those that a mesh axis runs over, the one named last changes fastest.
Arguments:
- hidden: bfloat16 [128, 36864], P(('groups', 'fsdp', 'sub'), 'mp'), parts along dimension 0, may hold values from -6 to 6
- residual: bfloat16 [128, 4608], P(('groups', 'fsdp', 'sub')), parts along dimension 0, may hold values from -6 to 6
- down_packed: int32 [4608, 4608], P('mp', 'fsdp'), may hold values from -2147483648 to 2147483646
- down_scale: bfloat16 [288, 4608], P('mp', 'fsdp'), may hold values from 0.00049972534 to 0.0019989014
- post_gain: float32 [4608], replicated, may hold values from 0.1 to 1.9
- final_gain: float32 [4608], replicated, may hold values from 0.1 to 1.9
- embed_packed: int32 [8192, 576], P(('fsdp', 'mp', 'sub')), may hold values from -2147483648 to 2147483646
- embed_scale: bfloat16 [8192, 36], P(('fsdp', 'mp', 'sub')), may hold values from 0.0059814453 to 0.029907227
- targets: int32 [128], P(('groups', 'fsdp', 'sub')), parts along dimension 0, may hold values from 0 to 8191
- loss_mask: int32 [128], P(('groups', 'fsdp', 'sub')), parts along dimension 0, may hold values 0 or 1
Outputs:
- token_loss: float32 [128], P(('groups', 'fsdp', 'sub')), parts along dimension 0
- mean_loss: float32 [2], P('groups'), parts along dimension 0
There are 2 independent parts, one for each index of `groups`. A program takes and returns all parts, laid end to end along the dimension named above; an argument that names none is the same for every part. Nothing has to cross between parts.
Inputs may be any that keep to these rules, and one draw needn't show every extreme that they name: `down_packed`: bits 4 k to 4 k + 3 of the word in row r hold the signed code of row 8 r + k of the down projection, k = 0..7. `embed_packed`: bits 4 k to 4 k + 3 of the word in column j hold the signed code of column k * 576 + j of the embedding, k = 0..7.
All inputs are finite; a program needn't handle non-finite values. No bound on the sum of `loss_mask` on one device may be relied on, other than what follows from the above.
Results may differ from a plain program's by a relative error of at most 0.00097.
Values may be sent and summed in bfloat16 or wider, within the bound.
A program may use at most 128 MiB of HBM per device.

v0:
```python
import jax
import jax.numpy as jnp
from jax import lax
from jax.sharding import PartitionSpec as P

EPS = 1e-06
CAP = 30.0


def signed_planes(words):
    shifts = (28 - 4 * jnp.arange(8, dtype=jnp.int32))[None, :, None]
    lifted = jnp.left_shift(words[:, None, :], shifts)
    return jnp.right_shift(lifted, 28)


def dequant_down(words, scales):
    cols = words.shape[1]
    codes = signed_planes(words).astype(jnp.bfloat16)
    grouped = codes.reshape(scales.shape[0], -1, cols) * scales[:, None, :]
    return grouped.reshape(-1, cols)


def dequant_embed(words, scales):
    rows = words.shape[0]
    codes = signed_planes(words).astype(jnp.bfloat16)
    grouped = codes.reshape(rows, scales.shape[1], -1) * scales[:, :, None]
    return grouped.reshape(rows, -1)


def normalize_rows(ffn, residual, post_gain, final_gain):
    ffn = lax.psum(ffn, "mp")
    normed = ffn * lax.rsqrt(jnp.mean(ffn * ffn, axis=-1, keepdims=True) + EPS) * post_gain
    stream = residual.astype(jnp.float32) + normed
    return (
        stream * lax.rsqrt(jnp.mean(stream * stream, axis=-1, keepdims=True) + EPS) * final_gain
    ).astype(jnp.bfloat16)


def on_device(
    hidden,
    residual,
    down_packed,
    down_scale,
    post_gain,
    final_gain,
    embed_packed,
    embed_scale,
    targets,
    loss_mask,
):
    tok_rows = hidden.shape[0]
    local_weight = dequant_down(down_packed, down_scale)
    partial_cols = jnp.dot(
        lax.all_gather(hidden, "fsdp", axis=0, tiled=True),
        local_weight,
        preferred_element_type=jnp.float32,
    )
    ffn = lax.all_to_all(partial_cols, "fsdp", split_axis=0, concat_axis=1, tiled=True)
    states = normalize_rows(ffn, residual, post_gain, final_gain)
    all_states, all_targets = (
        lax.all_gather(states, ("fsdp", "sub"), axis=0, tiled=True),
        lax.all_gather(targets, ("fsdp", "sub"), axis=0, tiled=True),
    )
    embed = dequant_embed(embed_packed, embed_scale)
    logits = lax.dot_general(
        all_states, embed, (((1,), (1,)), ((), ())), preferred_element_type=jnp.float32
    )
    capped = CAP * jnp.tanh(logits / CAP)
    vocab_rows = embed.shape[0]
    first_id = lax.axis_index(("fsdp", "mp", "sub")) * vocab_rows
    ids = first_id + jnp.arange(vocab_rows, dtype=jnp.int32)
    hits = all_targets[:, None] == ids[None, :]
    exp_sums, target_logits = lax.psum(
        (jnp.sum(jnp.exp(capped), axis=1), jnp.sum(jnp.where(hits, capped, 0.0), axis=1)),
        ("fsdp", "mp", "sub"),
    )
    own_start = lax.axis_index(("fsdp", "sub")) * tok_rows
    own_sums = lax.dynamic_slice_in_dim(exp_sums, own_start, tok_rows, 0)
    own_targets = lax.dynamic_slice_in_dim(target_logits, own_start, tok_rows, 0)
    weights = loss_mask.astype(jnp.float32)
    token_loss = weights * (jnp.log(own_sums) - own_targets)
    loss_sum, count = lax.psum((jnp.sum(token_loss), jnp.sum(weights)), ("fsdp", "sub"))
    mean_loss = (loss_sum / jnp.maximum(count, 1.0)).reshape(1)
    return (token_loss, mean_loss)


def solution(mesh):
    return jax.shard_map(
        on_device,
        mesh=mesh,
        in_specs=(
            P(("groups", "fsdp", "sub"), "mp"),
            P(("groups", "fsdp", "sub"), None),
            P("mp", "fsdp"),
            P("mp", "fsdp"),
            P(),
            P(),
            P(("fsdp", "mp", "sub"), None),
            P(("fsdp", "mp", "sub"), None),
            P(("groups", "fsdp", "sub")),
            P(("groups", "fsdp", "sub")),
        ),
        out_specs=(P(("groups", "fsdp", "sub")), P("groups")),
        check_vma=False,
    )
```

profile of v0, /device:TPU:0, one launch (start us, length us, event | category | flops | bytes accessed | tf_op | source)
XLA Modules:
  0.0 167.8 jit_solution(12297695420085963303)
XLA Ops:
  7.2 0.0 all-gather.2.cloned.1.call-start
  7.2 0.7 all-gather.2.cloned.1.call-update
  7.9 0.0 all-reduce.5.cloned.1.call-start
  8.0 0.1 shift_left.49
  8.1 17.8 %fusion.2 = bf16[18432,1152]{1,0:T(8,128)(2,1)} fusion(s32[18432]{0:T(1024)S(1)} %broadcast_bitcast_fusion, s32[2304,1152]{1,0:T(8,128)} %param.12, bf16[144,1152]{1,0:T(8,128)(2,1)} %param.13), kind=kLoop, calls=%fused_computation.3 | loop fusion | flops 148635648 | bytes 53489664 | tf_op jit(solution)/shard_map/mul | solution.py:19
  26.0 16.6 %all-gather.2.cloned.1.call-done = bf16[32,18432]{1,0:T(8,128)(2,1)} async-done(((bf16[8,18432]{1,0:T(8,128)(2,1)}), bf16[32,18432]{1,0:T(8,128)(2,1)}) %all-gather.2.cloned.1.call-update) | async-done | bytes 1179664 | tf_op jit(solution)/shard_map/all_gather | solution.py:54
  42.6 15.8 %convolution_bitcast_fusion = f32[4,8,1152]{2,1,0:T(8,128)S(1)} fusion(bf16[32,18432]{1,0:T(8,128)(2,1)} %all-gather.2.cloned.1.call-done, bf16[18432,1152]{1,0:T(8,128)(2,1)} %fusion.2), kind=kOutput, calls=%fused_computation.8 | convolution fusion | flops 1358954496 | bytes 43794432 | tf_op jit(solution)/shard_map/dot_general | solution.py:53
  58.4 9.7 %all_to_all.19 = f32[4,8,1152]{2,1,0:T(8,128)} all-to-all(f32[4,8,1152]{2,1,0:T(8,128)S(1)} %convolution_bitcast_fusion), channel_id=1, replica_groups=mesh['groups'=2,'fsdp'=4,'mp'=2,'sub'=2] {'fsdp'}, dimensions={0} | all-to-all | bytes 294912 | tf_op jit(solution)/shard_map/all_to_all | solution.py:58
  68.1 0.0 all-reduce.5.cloned.1.call-update
  68.1 0.1 shift_left.56
  68.2 0.1 shift_left.57
  68.3 0.6 dynamic-slice
  69.5 0.2 dynamic-update-slice
  69.8 3.6 %fusion.5 = bf16[512,4608]{0,1:T(8,128)(2,1)} fusion(s32[4608]{0:T(1024)S(1)} %shift_left.57, s32[512,576]{0,1:T(8,128)S(1)} %copy-done, bf16[512,36]{0,1:T(8,128)(2,1)S(1)} %copy-done.3), kind=kLoop, calls=%fused_computation.7 | loop fusion | flops 16515072 | bytes 5953536 | tf_op jit(solution)/shard_map/mul | solution.py:26
  73.4 6.5 %all-reduce = s32[64]{0:T(128)S(1)} all-reduce(s32[64]{0:T(128)S(1)} %dynamic-update-slice), channel_id=1, replica_groups=mesh['groups'=2,'fsdp'=4,'mp'=2,'sub'=2] {'fsdp','sub'}, use_global_device_ids=true, to_apply=%add | all-reduce | flops 64 | bytes 512
  79.8 8.8 %all-reduce.5.cloned.1.call-done = f32[8,4608]{1,0:T(8,128)} async-done(((f32[8,4608]{1,0:T(8,128)}), f32[8,4608]{1,0:T(8,128)}) %all-reduce.5.cloned.1.call-update) | async-done | bytes 147472 | tf_op jit(solution)/shard_map/psum | solution.py:31
  88.7 1.1 multiply_reduce_fusion.1
  89.8 1.1 multiply_reduce_fusion
  90.9 1.0 multiply_convert_fusion
  91.9 15.1 %all_gather.10 = bf16[64,4608]{1,0:T(8,128)(2,1)S(1)} all-gather(bf16[8,4608]{1,0:T(8,128)(2,1)S(1)} %multiply_convert_fusion), channel_id=1, replica_groups=mesh['groups'=2,'fsdp'=4,'mp'=2,'sub'=2] {'fsdp','sub'}, dimensions={0}, use_global_device_ids=true | all-gather | bytes 663552 | tf_op jit(solution)/shard_map/all_gather | solution.py:61
  107.0 3.4 %exponential_reduce_fusion = (f32[64]{0:T(128)S(1)}, f32[64]{0:T(128)S(1)}) fusion(s32[512]{0:T(512)S(1)} %iota_add_fusion, s32[64]{0:T(128)S(1)} %all-reduce, bf16[64,4608]{1,0:T(8,128)(2,1)S(1)} %all_gather.10, bf16[512,4608]{0,1:T(8,128)(2,1)} %fusion.5), kind=kOutput, calls=%fused_computation.17 | convolution fusion | flops 302186368 | bytes 5311232 | tf_op jit(solution)/shard_map/dot_general | solution.py:65
  110.4 32.7 %all-reduce.1 = (f32[64]{0:T(128)S(1)}, f32[64]{0:T(128)S(1)}) all-reduce(f32[64]{0:T(128)S(1)} %get-tuple-element.3, f32[64]{0:T(128)S(1)} %get-tuple-element.2), channel_id=1, replica_groups=mesh['groups'=2,'fsdp'=4,'mp'=2,'sub'=2] {'fsdp','mp','sub'}, use_global_device_ids=true, to_apply=%region_6.7 | all-reduce | flops 128 | bytes 1024 | tf_op jit(solution)/shard_map/psum | solution.py:73
  143.1 1.3 fusion.8
  144.4 14.2 %all-reduce.2 = (f32[]{:T(128)}, f32[]{:T(128)}) all-reduce(f32[]{:T(128)} %get-tuple-element.8, f32[]{:T(128)} %get-tuple-element.10), channel_id=1, replica_groups=mesh['groups'=2,'fsdp'=4,'mp'=2,'sub'=2] {'fsdp','sub'}, use_global_device_ids=true, to_apply=%region_8.9 | all-reduce | flops 2 | bytes 16 | tf_op jit(solution)/shard_map/psum | solution.py:82
  (23 shorter events, 0.1 us)
Async XLA Ops:
  7.2 35.4 %all-gather.2.cloned.1.call-start = ((), (), s32[]{:S(2)}) async-start(), calls=%async_computation.1 | async-start | bytes 1474560 | tf_op jit(solution)/shard_map/all_gather | solution.py:54
  7.9 80.8 %all-reduce.5.cloned.1.call-start = ((), (), s32[]{:S(2)}) async-start(), calls=%async_computation.2 | async-start | bytes 294912 | tf_op jit(solution)/shard_map/psum | solution.py:31
  25.9 42.4 %copy-start.7 = (u32[32]{0:T(128)S(1)}, u32[32]{0:T(128)}, u32[]{:S(2)}) copy-start(u32[32]{0:T(128)} %constant.48) | copy-start | bytes 388
  25.9 43.6 %copy-start.6 = (s32[8]{0:T(128)S(1)}, s32[8]{0:T(128)}, u32[]{:S(2)}) copy-start(s32[8]{0:T(128)} %param.18) | copy-start | bytes 100
  25.9 43.9 %copy-start = (s32[512,576]{0,1:T(8,128)S(1)}, s32[512,576]{0,1:T(8,128)}, u32[]{:S(2)}) copy-start(s32[512,576]{0,1:T(8,128)} %param.16) | copy-start | bytes 3538948
  25.9 43.8 %copy-start.3 = (bf16[512,36]{0,1:T(8,128)(2,1)S(1)}, bf16[512,36]{0,1:T(8,128)(2,1)}, u32[]{:S(2)}) copy-start(bf16[512,36]{0,1:T(8,128)(2,1)} %param.17) | copy-start | bytes 110596
  26.0 63.8 %copy-start.1 = (bf16[8,4608]{1,0:T(8,128)(2,1)S(1)}, bf16[8,4608]{1,0:T(8,128)(2,1)}, u32[]{:S(2)}) copy-start(bf16[8,4608]{1,0:T(8,128)(2,1)} %param.11) | copy-start | bytes 221188
  26.0 63.8 %copy-start.2 = (f32[4608]{0:T(1024)S(1)}, f32[4608]{0:T(1024)}, u32[]{:S(2)}) copy-start(f32[4608]{0:T(1024)} %param.14) | copy-start | bytes 55300
  26.0 64.9 %copy-start.4 = (f32[4608]{0:T(1024)S(1)}, f32[4608]{0:T(1024)}, u32[]{:S(2)}) copy-start(f32[4608]{0:T(1024)} %param.15) | copy-start | bytes 55300
  58.4 84.8 %copy-start.5 = (s32[8]{0:T(128)S(1)}, s32[8]{0:T(128)}, u32[]{:S(2)}) copy-start(s32[8]{0:T(128)} %param.19) | copy-start | bytes 100
Sparse Core Ops, SparseCore 0:
  9.5 32.9 all-gather.1
  68.2 20.3 all-reduce.4
where the time goes:
time: 168 us
  blocking collectives  78.2 us (47%)
  waiting for transfers between devices  26.1 us (16%)
  other arithmetic  25.9 us (15%)
  matrix products  19.2 us (11%)
  between operations  17.2 us (10%)
    psum x1, blocking collectives, on_device(): lax.psum((jnp.sum(jnp.exp(capped), axis=1), jnp.sum(jnp.where(hits, cappe...  32.7 us
    mul x1, other arithmetic, dequant_down(): grouped = codes.reshape(scales.shape[0], -1, cols) * scales[:, None, :]  17.8 us
    all_gather x1, waiting for transfers between devices, on_device(): lax.all_gather(hidden, 'fsdp', axis=0, tiled=True)  16.6 us
    dot_general x1, matrix products, on_device(): jnp.dot(lax.all_gather(hidden, 'fsdp', axis=0, tiled=True), local_weight,...  15.8 us
    all_gather x1, blocking collectives, on_device(): lax.all_gather(states, ('fsdp', 'sub'), axis=0, tiled=True)  15.1 us
    psum x1, blocking collectives, on_device(): lax.psum((jnp.sum(token_loss), jnp.sum(weights)), ('fsdp', 'sub'))  14.2 us
    all_to_all x1, blocking collectives, on_device(): lax.all_to_all(partial_cols, 'fsdp', split_axis=0, concat_axis=1, tiled=T...  9.71 us
    psum x1, waiting for transfers between devices, normalize_rows(): ffn = lax.psum(ffn, 'mp')  8.84 us
  transfers between devices with their start and end apart: 2, of which 2 were waited for; matrix products, arithmetic and copies ran while one was open for 13% of the time, Pallas kernels for 0%

commit v1 on v0

--- a/solution.py
+++ b/solution.py
@@ -58,7 +58,12 @@
     ffn = lax.all_to_all(partial_cols, "fsdp", split_axis=0, concat_axis=1, tiled=True)
     states = normalize_rows(ffn, residual, post_gain, final_gain)
     all_states, all_targets = (
-        lax.all_gather(states, ("fsdp", "sub"), axis=0, tiled=True),
+        jnp.concatenate(
+            lax.all_to_all(
+                jnp.stack([states] * lax.axis_size(("fsdp", "sub"))), ("fsdp", "sub"), 0, 0
+            ),
+            axis=0,
+        ),
         lax.all_gather(targets, ("fsdp", "sub"), axis=0, tiled=True),
     )
     embed = dequant_embed(embed_packed, embed_scale)

time: 168 us -> 178 us (1.060)
  waiting for transfers between devices: 26.1 us -> 37.8 us
  blocking collectives: 78.2 us -> 69.6 us
  starting transfers between devices: 0.08 us -> 4.68 us
  local copies, waits for them, and re-layouts: 1.12 us -> 3.18 us
    all_gather x1 -> x0, blocking collectives: 15.1 us -> none  [on_device(): lax.all_gather(states, ('fsdp', 'sub'), axis=0, tiled=True)]
    psum x1, waiting for transfers between devices: 8.84 us -> 20.6 us  [normalize_rows(): ffn = lax.psum(ffn, 'mp')]
    unnamed x1, blocking collectives: 6.46 us -> 15.3 us
    all_to_all x0 -> x1, starting transfers between devices: none -> 4.61 us  [on_device(): lax.all_to_all(jnp.stack([states] * lax.axis_size(('fsdp', 'sub'))), ('fs...]
    psum x1, blocking collectives: 32.7 us -> 30.4 us  [on_device(): lax.psum((jnp.sum(jnp.exp(capped), axis=1), jnp.sum(jnp.where(hits, cappe...]
  transfers between devices with their start and end apart: 2 -> 3, of which waited for: 2 -> 2; matrix products, arithmetic and copies ran while one was open for 13% -> 13% of each run, Pallas kernels for 0% -> 0%
where the time goes in v1:
time: 178 us
  blocking collectives  69.6 us (39%)
  waiting for transfers between devices  37.8 us (21%)
  other arithmetic  25.9 us (15%)
  matrix products  19.2 us (11%)
  between operations  17.2 us (10%)
  starting transfers between devices  4.68 us (3%)
  local copies, waits for them, and re-layouts  3.18 us (2%)
    psum x1, blocking collectives, on_device(): lax.psum((jnp.sum(jnp.exp(capped), axis=1), jnp.sum(jnp.where(hits, cappe...  30.4 us
    psum x1, waiting for transfers between devices, normalize_rows(): ffn = lax.psum(ffn, 'mp')  20.6 us
    mul x1, other arithmetic, dequant_down(): grouped = codes.reshape(scales.shape[0], -1, cols) * scales[:, None, :]  17.8 us
    all_gather x1, waiting for transfers between devices, on_device(): lax.all_gather(hidden, 'fsdp', axis=0, tiled=True)  16.6 us
    dot_general x1, matrix products, on_device(): jnp.dot(lax.all_gather(hidden, 'fsdp', axis=0, tiled=True), local_weight,...  15.8 us
    unnamed x1, blocking collectives  15.3 us
    psum x1, blocking collectives, on_device(): lax.psum((jnp.sum(token_loss), jnp.sum(weights)), ('fsdp', 'sub'))  14.2 us
    all_to_all x1, blocking collectives, on_device(): lax.all_to_all(partial_cols, 'fsdp', split_axis=0, concat_axis=1, tiled=T...  9.71 us
  transfers between devices with their start and end apart: 3, of which 2 were waited for; matrix products, arithmetic and copies ran while one was open for 13% of the time, Pallas kernels for 0%

profile of v1, /device:TPU:0, one launch (start us, length us, event | category | flops | bytes accessed | tf_op | source)
XLA Modules:
  0.0 177.6 jit_solution(14367403783102617484)
XLA Ops:
  7.2 0.7 all-gather.2.cloned.1.call-update
  7.9 0.0 all-reduce.5.cloned.1.call-start
  8.0 0.1 shift_left.56
  8.1 17.8 %fusion.2 = bf16[18432,1152]{1,0:T(8,128)(2,1)} fusion(s32[18432]{0:T(1024)S(1)} %broadcast_bitcast_fusion, s32[2304,1152]{1,0:T(8,128)} %param.12, bf16[144,1152]{1,0:T(8,128)(2,1)} %param.13), kind=kLoop, calls=%fused_computation.3 | loop fusion | flops 148635648 | bytes 53489664 | tf_op jit(solution)/shard_map/mul | solution.py:19
  26.0 16.6 %all-gather.2.cloned.1.call-done = bf16[32,18432]{1,0:T(8,128)(2,1)} async-done(((bf16[8,18432]{1,0:T(8,128)(2,1)}), bf16[32,18432]{1,0:T(8,128)(2,1)}) %all-gather.2.cloned.1.call-update) | async-done | bytes 1179664 | tf_op jit(solution)/shard_map/all_gather | solution.py:54
  42.6 15.8 %convolution_bitcast_fusion = f32[4,8,1152]{2,1,0:T(8,128)S(1)} fusion(bf16[32,18432]{1,0:T(8,128)(2,1)} %all-gather.2.cloned.1.call-done, bf16[18432,1152]{1,0:T(8,128)(2,1)} %fusion.2), kind=kOutput, calls=%fused_computation.6 | convolution fusion | flops 1358954496 | bytes 43794432 | tf_op jit(solution)/shard_map/dot_general | solution.py:53
  58.4 9.7 %all_to_all.24 = f32[4,8,1152]{2,1,0:T(8,128)} all-to-all(f32[4,8,1152]{2,1,0:T(8,128)S(1)} %convolution_bitcast_fusion), channel_id=1, replica_groups=mesh['groups'=2,'fsdp'=4,'mp'=2,'sub'=2] {'fsdp'}, dimensions={0} | all-to-all | bytes 294912 | tf_op jit(solution)/shard_map/all_to_all | solution.py:58
  68.1 20.6 %all-reduce.5.cloned.1.call-done = f32[8,4608]{1,0:T(8,128)} async-done(((f32[8,4608]{1,0:T(8,128)}), f32[8,4608]{1,0:T(8,128)}) %all-reduce.5.cloned.1.call-update) | async-done | bytes 147472 | tf_op jit(solution)/shard_map/psum | solution.py:31
  88.7 1.1 multiply_reduce_fusion.1
  89.8 1.1 multiply_reduce_fusion
  90.9 1.0 multiply_convert_fusion
  91.9 0.9 stack.2
  92.8 4.6 %all-to-all-start.1 = ((bf16[8,8,4608]{2,1,0:T(8,128)(2,1)}), bf16[8,8,4608]{2,1,0:T(8,128)(2,1)S(1)}, u32[]{:S(2)}, u32[]{:S(2)}) async-start(bf16[8,8,4608]{2,1,0:T(8,128)(2,1)} %stack.2), calls=%async_computation.1 | async-start | bytes 1179648 | tf_op jit(solution)/shard_map/all_to_all | solution.py:62
  97.4 0.1 shift_left.63
  97.5 0.1 shift_left.64
  97.6 0.6 dynamic-slice
  98.8 0.2 dynamic-update-slice
  99.1 15.3 %all-reduce = s32[64]{0:T(128)S(1)} all-reduce(s32[64]{0:T(128)S(1)} %dynamic-update-slice), channel_id=1, replica_groups=mesh['groups'=2,'fsdp'=4,'mp'=2,'sub'=2] {'fsdp','sub'}, use_global_device_ids=true, to_apply=%add | all-reduce | flops 64 | bytes 512
  114.3 1.2 shift_left.61
  115.6 3.5 %fusion.3 = bf16[512,36,128]{0,2,1:T(8,128)(2,1)} fusion(s32[512,36,128]{0,2,1:T(8,128)S(1)} %bitcast.31, s32[36,128]{1,0:T(8,128)S(1)} %shift_left.64, bf16[512,36]{0,1:T(8,128)(2,1)S(1)} %copy-done.3), kind=kLoop, calls=%fused_computation.5 | loop fusion | flops 16515072 | bytes 14211072 | tf_op jit(solution)/shard_map/mul | solution.py:26
  119.1 3.4 %exponential_reduce_fusion = (f32[64]{0:T(128)S(1)}, f32[64]{0:T(128)S(1)}) fusion(s32[512]{0:T(512)S(1)} %iota_add_fusion, s32[64]{0:T(128)S(1)} %all-reduce, bf16[512,4608]{0,1:T(8,128)(2,1)} %bitcast.32, bf16[8,8,4608]{2,1,0:T(8,128)(2,1)S(1)} %all-to-all-done.1), kind=kOutput, calls=%fused_computation.16 | convolution fusion | flops 302186368 | bytes 5311232 | tf_op jit(solution)/shard_map/dot_general | solution.py:70
  122.5 30.4 %all-reduce.1 = (f32[64]{0:T(128)S(1)}, f32[64]{0:T(128)S(1)}) all-reduce(f32[64]{0:T(128)S(1)} %get-tuple-element.3, f32[64]{0:T(128)S(1)} %get-tuple-element.2), channel_id=1, replica_groups=mesh['groups'=2,'fsdp'=4,'mp'=2,'sub'=2] {'fsdp','mp','sub'}, use_global_device_ids=true, to_apply=%region_6.7 | all-reduce | flops 128 | bytes 1024 | tf_op jit(solution)/shard_map/psum | solution.py:78
  152.9 1.3 fusion.7
  154.2 14.2 %all-reduce.2 = (f32[]{:T(128)}, f32[]{:T(128)}) all-reduce(f32[]{:T(128)} %get-tuple-element.8, f32[]{:T(128)} %get-tuple-element.10), channel_id=1, replica_groups=mesh['groups'=2,'fsdp'=4,'mp'=2,'sub'=2] {'fsdp','sub'}, use_global_device_ids=true, to_apply=%region_8.9 | all-reduce | flops 2 | bytes 16 | tf_op jit(solution)/shard_map/psum | solution.py:87
  (26 shorter events, 0.1 us)
Async XLA Ops:
  7.2 35.4 %all-gather.2.cloned.1.call-start = ((), (), s32[]{:S(2)}) async-start(), calls=%async_computation.2 | async-start | bytes 1474560 | tf_op jit(solution)/shard_map/all_gather | solution.py:54
  7.9 80.8 %all-reduce.5.cloned.1.call-start = ((), (), s32[]{:S(2)}) async-start(), calls=%async_computation.3 | async-start | bytes 294912 | tf_op jit(solution)/shard_map/psum | solution.py:31
  25.9 63.8 %copy-start.1 = (bf16[8,4608]{1,0:T(8,128)(2,1)S(1)}, bf16[8,4608]{1,0:T(8,128)(2,1)}, u32[]{:S(2)}) copy-start(bf16[8,4608]{1,0:T(8,128)(2,1)} %param.11) | copy-start | bytes 221188
  25.9 63.8 %copy-start.2 = (f32[4608]{0:T(1024)S(1)}, f32[4608]{0:T(1024)}, u32[]{:S(2)}) copy-start(f32[4608]{0:T(1024)} %param.14) | copy-start | bytes 55300
  25.9 65.0 %copy-start.4 = (f32[4608]{0:T(1024)S(1)}, f32[4608]{0:T(1024)}, u32[]{:S(2)}) copy-start(f32[4608]{0:T(1024)} %param.15) | copy-start | bytes 55300
  25.9 71.6 %copy-start.7 = (u32[32]{0:T(128)S(1)}, u32[32]{0:T(128)}, u32[]{:S(2)}) copy-start(u32[32]{0:T(128)} %constant.48) | copy-start | bytes 388
  26.0 72.8 %copy-start.6 = (s32[8]{0:T(128)S(1)}, s32[8]{0:T(128)}, u32[]{:S(2)}) copy-start(s32[8]{0:T(128)} %param.18) | copy-start | bytes 100
  26.0 88.4 %copy-start = (s32[512,576]{0,1:T(8,128)S(1)}, s32[512,576]{0,1:T(8,128)}, u32[]{:S(2)}) copy-start(s32[512,576]{0,1:T(8,128)} %param.16) | copy-start | bytes 3538948
  58.4 57.2 %copy-start.3 = (bf16[512,36]{0,1:T(8,128)(2,1)S(1)}, bf16[512,36]{0,1:T(8,128)(2,1)}, u32[]{:S(2)}) copy-start(bf16[512,36]{0,1:T(8,128)(2,1)} %param.17) | copy-start | bytes 110596
  92.8 26.3 %all-to-all-start.1 = ((bf16[8,8,4608]{2,1,0:T(8,128)(2,1)}), bf16[8,8,4608]{2,1,0:T(8,128)(2,1)S(1)}, u32[]{:S(2)}, u32[]{:S(2)}) async-start(bf16[8,8,4608]{2,1,0:T(8,128)(2,1)} %stack.2), calls=%async_computation.1 | async-start | bytes 1179648 | tf_op jit(solution)/shard_map/all_to_all | solution.py:62
  115.5 37.4 %copy-start.5 = (s32[8]{0:T(128)S(1)}, s32[8]{0:T(128)}, u32[]{:S(2)}) copy-start(s32[8]{0:T(128)} %param.19) | copy-start | bytes 100
Sparse Core Ops, SparseCore 0:
  9.5 32.9 all-gather.1
  68.2 20.3 all-reduce.4
